TPU v7x, 32 devices: a whole 2x2x4 slice. The times are simulated.
32 devices in a mesh: row: 4 (over y, x), col: 8 (over z, core).
Axes of the slice: x: 2, y: 2, z: 4, core: 2. Of those that a mesh axis runs over, the one named last changes fastest.
Arguments:
- pair_window: bfloat16 [8, 16, 32, 128], P('col', 'row'), may hold values from -6 to 6
- tri_cotangent: bfloat16 [8, 16, 128, 128], P(None, 'row', 'col'), may hold values from -0.75 to 0.75
- saved_left: bfloat16 [8, 16, 32, 128], P('col', 'row'), may hold values from -6 to 6
- saved_right: bfloat16 [8, 16, 32, 128], P('col', 'row'), may hold values from -6 to 6
- norm_gain: float32 [128], replicated, may hold values from 0.5 to 1.5
- norm_bias: float32 [128], replicated, may hold values from -3 to 3
- proj_weight: bfloat16 [4, 128, 128], replicated, may hold values from -0.5 to 0.5
Outputs:
- pair_grad: bfloat16 [8, 16, 32, 128], P('col', 'row')
- weight_grad: float32 [4, 128, 128], replicated
- norm_grad: float32 [2, 128], replicated
All inputs are finite; a program needn't handle non-finite values.
Results may differ from a plain program's by a relative error of at most 0.0085.
Values may be sent and summed in bfloat16 or wider, within the bound.
A program may use at most 64 MiB of HBM per device.

v0:
```python
import jax
import jax.numpy as jnp
from jax import lax
from jax.sharding import PartitionSpec as P


def gated_norm_back(pair_rows, left_grad, right_grad, norm_gain, norm_bias, proj_weight):
    pair = pair_rows.astype(jnp.float32)
    average = jnp.mean(pair, axis=-1, keepdims=True)
    centred = pair - average
    variance = jnp.mean(centred * centred, axis=-1, keepdims=True)
    inv_std = lax.rsqrt(variance + 1e-05)
    unit_pair = centred * inv_std
    normed = (unit_pair * norm_gain + norm_bias).astype(jnp.bfloat16)
    chans = proj_weight.shape[2]
    stacked = jnp.transpose(proj_weight, (1, 0, 2)).reshape(proj_weight.shape[1], 4 * chans)
    preact = jnp.dot(normed, stacked, preferred_element_type=jnp.float32)
    gate_left = jax.nn.sigmoid(preact[:, :chans])
    value_left = preact[:, chans : 2 * chans]
    gate_right = jax.nn.sigmoid(preact[:, 2 * chans : 3 * chans])
    value_right = preact[:, 3 * chans :]
    pre_grads = jnp.concatenate(
        [
            left_grad * value_left * gate_left * (1.0 - gate_left),
            left_grad * gate_left,
            right_grad * value_right * gate_right * (1.0 - gate_right),
            right_grad * gate_right,
        ],
        axis=1,
    ).astype(jnp.bfloat16)
    weight_part = lax.dot_general(
        normed, pre_grads, (((0,), (0,)), ((), ())), preferred_element_type=jnp.float32
    )
    weight_part = jnp.transpose(weight_part.reshape(proj_weight.shape[1], 4, chans), (1, 0, 2))
    normed_grad = jnp.dot(pre_grads, stacked.T, preferred_element_type=jnp.float32)
    norm_part = jnp.stack([jnp.sum(normed_grad * unit_pair, axis=0), jnp.sum(normed_grad, axis=0)])
    scaled_grad = normed_grad * norm_gain
    pair_grad = inv_std * (
        scaled_grad
        - jnp.mean(scaled_grad, axis=-1, keepdims=True)
        - unit_pair * jnp.mean(scaled_grad * unit_pair, axis=-1, keepdims=True)
    )
    return (pair_grad.astype(jnp.bfloat16), weight_part, norm_part)


def on_device(
    pair_window, tri_cotangent, saved_left, saved_right, norm_gain, norm_bias, proj_weight
):
    block_count, own_rows, col_tokens, channels = tri_cotangent.shape
    window_len = saved_left.shape[2]
    right_rows = lax.all_gather(saved_right, "row", axis=1, tiled=True)[0]
    cot_flat = tri_cotangent.reshape(block_count * own_rows, col_tokens, channels)
    cot_piece = cot_flat
    left_grad = lax.psum_scatter(
        jnp.einsum("ijh,jkh->ikh", cot_piece, right_rows, preferred_element_type=jnp.float32),
        "col",
        scatter_dimension=0,
        tiled=True,
    )
    left_rows = lax.all_gather(saved_left, "col", axis=0, tiled=True)
    left_flat = left_rows.reshape(block_count * own_rows, window_len, channels)
    cot_piece = cot_flat
    right_grad = lax.psum_scatter(
        jnp.einsum("ijh,ikh->jkh", cot_piece, left_flat, preferred_element_type=jnp.float32),
        "row",
        scatter_dimension=0,
        tiled=True,
    )
    positions = own_rows * window_len
    pair_grad, weight_part, norm_part = gated_norm_back(
        pair_window.reshape(positions, pair_window.shape[3]),
        left_grad.reshape(positions, channels),
        right_grad.reshape(positions, channels),
        norm_gain,
        norm_bias,
        proj_weight,
    )
    weight_grad, norm_grad = lax.psum((weight_part, norm_part), ("row", "col"))
    return (pair_grad.reshape(pair_window.shape), weight_grad, norm_grad)


def solution(mesh):
    return jax.shard_map(
        on_device,
        mesh=mesh,
        in_specs=(
            P("col", "row", None, None),
            P(None, "row", "col", None),
            P("col", "row", None, None),
            P("col", "row", None, None),
            P(),
            P(),
            P(),
        ),
        out_specs=(P("col", "row", None, None), P(), P()),
        check_vma=False,
    )
```

profile of v0, /device:TPU:0, one launch (start us, length us, event | category | flops | bytes accessed | tf_op | source)
XLA Modules:
  0.0 225.6 jit_solution(12033966803922568109)
XLA Ops:
  7.2 1.4 copy.28
  8.6 16.1 %all_gather.7 = bf16[8,4,32,128]{3,2,1,0:T(8,128)(2,1)S(1)} all-gather(bf16[1,4,32,128]{3,2,1,0:T(8,128)(2,1)} %param.9), channel_id=1, replica_groups=mesh['row'=4,'col'=8] {'col'}, dimensions={0}, use_global_device_ids=true | all-gather | bytes 294912 | tf_op jit(solution)/shard_map/all_gather | solution.py:60
  24.8 0.9 copy.31
  25.7 0.4 convolution_bitcast_fusion.1
  26.1 1.1 copy.33
  27.3 8.5 %all_gather.6 = bf16[1,16,32,128]{3,2,0,1:T(8,128)(2,1)S(1)} all-gather(bf16[1,4,32,128]{3,2,0,1:T(8,128)(2,1)S(1)} %bitcast.59), channel_id=1, replica_groups=mesh['row'=4,'col'=8] {'row'}, dimensions={1}, use_global_device_ids=true | all-gather | bytes 163840 | tf_op jit(solution)/shard_map/all_gather | solution.py:51
  35.8 0.4 copy.27
  36.2 0.5 convolution_bitcast_fusion
  36.8 2.2 copy.29
  39.1 0.1 convert_reduce_fusion
  39.3 0.2 multiply_reduce_fusion.2
  39.6 0.1 copy.30
  39.7 0.1 add_convert_fusion
  39.8 0.2 fusion.19
  40.0 12.8 %reduce-scatter.5.cloned.1.call-done = f32[4,32,128]{2,1,0:T(8,128)} async-done(((f32[16,32,128]{2,1,0:T(8,128)}), f32[4,32,128]{2,1,0:T(8,128)}) %reduce-scatter.5.cloned.1.call-update) | async-done | bytes 65552 | tf_op jit(solution)/shard_map/reduce_scatter | solution.py:63
  52.8 33.6 %reduce-scatter.3.cloned.1.call-done = f32[4,32,128]{2,1,0:T(8,128)} async-done(((f32[32,32,128]{2,1,0:T(8,128)}), f32[4,32,128]{2,1,0:T(8,128)}) %reduce-scatter.3.cloned.1.call-update) | async-done | bytes 65552 | tf_op jit(solution)/shard_map/reduce_scatter | solution.py:54
  86.4 0.9 fusion.12
  87.4 0.1 copy.38
  87.5 0.9 convolution_bitcast_fusion.2
  88.4 0.3 multiply_reduce_fusion
  88.7 37.9 %psum.15 = f32[2,128]{1,0:T(2,128)} all-reduce(f32[2,128]{1,0:T(2,128)S(1)} %pad_maximum_fusion.2), channel_id=1, replica_groups=mesh['row'=4,'col'=8] {'row','col'}, use_global_device_ids=true, to_apply=%region_9.0 | all-reduce | flops 256 | bytes 2048 | tf_op jit(solution)/shard_map/psum | solution.py:78
  126.6 0.8 multiply_convert_fusion
  127.4 90.0 %all-reduce.2.cloned.1.call-done = f32[4,128,128]{2,1,0:T(8,128)} async-done(((f32[4,128,128]{2,1,0:T(8,128)}), f32[4,128,128]{2,1,0:T(8,128)}) %all-reduce.2.cloned.1.call-update) | async-done | bytes 262160 | tf_op jit(solution)/shard_map/psum | solution.py:78
  217.5 1.7 copy.40
  (23 shorter events, 0.4 us)
Async XLA Ops:
  7.2 45.6 %reduce-scatter.5.cloned.1.call-start = ((), (), s32[]{:S(2)}) async-start(), calls=%async_computation.3 | async-start | bytes 327680 | tf_op jit(solution)/shard_map/reduce_scatter | solution.py:63
  25.7 1.6 copy-start.2
  27.3 59.1 %reduce-scatter.3.cloned.1.call-start = ((), (), s32[]{:S(2)}) async-start(), calls=%async_computation.2 | async-start | bytes 589824 | tf_op jit(solution)/shard_map/reduce_scatter | solution.py:54
  36.8 2.3 %copy-start = (bf16[1,4,32,128]{3,2,1,0:T(8,128)(2,1)S(1)}, bf16[1,4,32,128]{3,2,1,0:T(8,128)(2,1)}, u32[]{:S(2)}) copy-start(bf16[1,4,32,128]{3,2,1,0:T(8,128)(2,1)} %param.7) | copy-start | bytes 98308
  36.8 2.8 %copy-start.1 = (bf16[4,128,128]{2,1,0:T(8,128)(2,1)S(1)}, bf16[4,128,128]{2,1,0:T(8,128)(2,1)}, u32[]{:S(2)}) copy-start(bf16[4,128,128]{2,1,0:T(8,128)(2,1)} %param.13) | copy-start | bytes 393220
  36.8 2.9 %copy-start.3 = (f32[128]{0:T(128)S(1)}, f32[128]{0:T(128)}, u32[]{:S(2)}) copy-start(f32[128]{0:T(128)} %param.11) | copy-start | bytes 1540
  36.8 2.9 %copy-start.4 = (f32[128]{0:T(128)S(1)}, f32[128]{0:T(128)}, u32[]{:S(2)}) copy-start(f32[128]{0:T(128)} %param.12) | copy-start | bytes 1540
  39.0 178.4 %all-reduce.2.cloned.1.call-start = ((), (), s32[]{:S(2)}) async-start(), calls=%async_computation.4 | async-start | bytes 524288 | tf_op jit(solution)/shard_map/psum | solution.py:78
Sparse Core Ops, SparseCore 0:
  27.4 25.3 reduce-scatter.4
  55.0 31.3 reduce-scatter.2
  92.5 124.9 all-reduce.1
where the time goes:
time: 226 us
  waiting for transfers between devices  136 us (60%)
  blocking collectives  62.5 us (28%)
  between operations  13.9 us (6%)
  local copies, waits for them, and re-layouts  8.23 us (4%)
  matrix products  2.3 us (1%)
    psum x1, waiting for transfers between devices, on_device(): weight_grad, norm_grad = lax.psum((weight_part, norm_part), ('row', 'col'))  90 us
    psum x1, blocking collectives, on_device(): weight_grad, norm_grad = lax.psum((weight_part, norm_part), ('row', 'col'))  37.9 us
    reduce_scatter x1, waiting for transfers between devices, on_device(): lax.psum_scatter(jnp.einsum('ijh,jkh->ikh', cot_piece, right_rows, prefer...  33.6 us
    all_gather x1, blocking collectives, on_device(): left_rows = lax.all_gather(saved_left, 'col', axis=0, tiled=True)  16.1 us
    reduce_scatter x1, waiting for transfers between devices, on_device(): lax.psum_scatter(jnp.einsum('ijh,ikh->jkh', cot_piece, left_flat, preferr...  12.8 us
    all_gather x1, blocking collectives, on_device(): right_rows = lax.all_gather(saved_right, 'row', axis=1, tiled=True)[0]  8.46 us
  transfers between devices with their start and end apart: 3, of which 3 were waited for; matrix products, arithmetic and copies ran while one was open for 2% of the time, Pallas kernels for 0%

commit v1 on v0

--- a/solution.py
+++ b/solution.py
@@ -75,7 +75,7 @@
         norm_bias,
         proj_weight,
     )
-    weight_grad, norm_grad = lax.psum((weight_part, norm_part), ("row", "col"))
+    weight_grad, norm_grad = lax.psum(lax.psum((weight_part, norm_part), "col"), "row")
     return (pair_grad.reshape(pair_window.shape), weight_grad, norm_grad)
 
 

time: 226 us -> 196 us (0.87)
  waiting for transfers between devices: 136 us -> 121 us
  blocking collectives: 62.5 us -> 48.7 us
    psum x1 -> x2, waiting for transfers between devices: 90 us -> 74.3 us  [the longest x1 54.2 us: on_device(): lax.psum((weight_part, norm_part), 'col')]
    psum x1 -> x2, blocking collectives: 37.9 us -> 24.1 us  [the longest x1 13.7 us: on_device(): lax.psum((weight_part, norm_part), 'col')]
  transfers between devices with their start and end apart: 3 -> 4, of which waited for: 3 -> 4; matrix products, arithmetic and copies ran while one was open for 2% -> 3% of each run, Pallas kernels for 0% -> 0%
where the time goes in v1:
time: 196 us
  waiting for transfers between devices  121 us (62%)
  blocking collectives  48.7 us (25%)
  between operations  13.9 us (7%)
  local copies, waits for them, and re-layouts  8.23 us (4%)
  matrix products  2.3 us (1%)
  other arithmetic  2.08 us (1%)
    psum x1, waiting for transfers between devices, on_device(): lax.psum((weight_part, norm_part), 'col')  54.2 us
    reduce_scatter x1, waiting for transfers between devices, on_device(): lax.psum_scatter(jnp.einsum('ijh,jkh->ikh', cot_piece, right_rows, prefer...  33.6 us
    psum x1, waiting for transfers between devices, on_device(): lax.psum(lax.psum((weight_part, norm_part), 'col'), 'row')  20 us
    all_gather x1, blocking collectives, on_device(): left_rows = lax.all_gather(saved_left, 'col', axis=0, tiled=True)  16.1 us
    psum x1, blocking collectives, on_device(): lax.psum((weight_part, norm_part), 'col')  13.7 us
    reduce_scatter x1, waiting for transfers between devices, on_device(): lax.psum_scatter(jnp.einsum('ijh,ikh->jkh', cot_piece, left_flat, preferr...  12.8 us
    psum x1, blocking collectives, on_device(): lax.psum(lax.psum((weight_part, norm_part), 'col'), 'row')  10.4 us
    all_gather x1, blocking collectives, on_device(): right_rows = lax.all_gather(saved_right, 'row', axis=1, tiled=True)[0]  8.46 us
  transfers between devices with their start and end apart: 4, of which 4 were waited for; matrix products, arithmetic and copies ran while one was open for 3% of the time, Pallas kernels for 0%

profile of v1, /device:TPU:0, one launch (start us, length us, event | category | flops | bytes accessed | tf_op | source)
XLA Modules:
  0.0 196.1 jit_solution(15850223264187886144)
XLA Ops:
  7.2 1.4 copy.28
  8.6 16.1 %all_gather.7 = bf16[8,4,32,128]{3,2,1,0:T(8,128)(2,1)S(1)} all-gather(bf16[1,4,32,128]{3,2,1,0:T(8,128)(2,1)} %param.9), channel_id=1, replica_groups=mesh['row'=4,'col'=8] {'col'}, dimensions={0}, use_global_device_ids=true | all-gather | bytes 294912 | tf_op jit(solution)/shard_map/all_gather | solution.py:60
  24.8 0.9 copy.31
  25.7 0.4 convolution_bitcast_fusion.1
  26.1 1.1 copy.33
  27.3 8.5 %all_gather.6 = bf16[1,16,32,128]{3,2,0,1:T(8,128)(2,1)S(1)} all-gather(bf16[1,4,32,128]{3,2,0,1:T(8,128)(2,1)S(1)} %bitcast.59), channel_id=1, replica_groups=mesh['row'=4,'col'=8] {'row'}, dimensions={1}, use_global_device_ids=true | all-gather | bytes 163840 | tf_op jit(solution)/shard_map/all_gather | solution.py:51
  35.8 0.4 copy.27
  36.2 0.5 convolution_bitcast_fusion
  36.8 2.2 %copy.29 = f32[32,32,128]{2,1,0:T(8,128)} copy(f32[32,32,128]{0,1,2:T(8,128)S(1)} %convolution_bitcast_fusion) | data formatting | bytes 1048576 | tf_op jit(solution)/shard_map/ijh,jkh->ikh/transpose | solution.py:55
  39.3 0.2 multiply_reduce_fusion.2
  39.6 0.1 copy.30
  39.8 0.2 fusion.19
  40.0 12.8 %reduce-scatter.5.cloned.1.call-done = f32[4,32,128]{2,1,0:T(8,128)} async-done(((f32[16,32,128]{2,1,0:T(8,128)}), f32[4,32,128]{2,1,0:T(8,128)}) %reduce-scatter.5.cloned.1.call-update) | async-done | bytes 65552 | tf_op jit(solution)/shard_map/reduce_scatter | solution.py:63
  52.8 33.6 %reduce-scatter.3.cloned.1.call-done = f32[4,32,128]{2,1,0:T(8,128)} async-done(((f32[32,32,128]{2,1,0:T(8,128)}), f32[4,32,128]{2,1,0:T(8,128)}) %reduce-scatter.3.cloned.1.call-update) | async-done | bytes 65552 | tf_op jit(solution)/shard_map/reduce_scatter | solution.py:54
  86.4 0.9 fusion.12
  87.4 0.1 copy.38
  87.5 0.9 convolution_bitcast_fusion.2
  88.5 0.3 multiply_reduce_fusion
  88.8 54.2 %all-reduce.3.cloned.1.call-done = f32[4,128,128]{2,1,0:T(8,128)} async-done(((f32[4,128,128]{2,1,0:T(8,128)}), f32[4,128,128]{2,1,0:T(8,128)}) %all-reduce.3.cloned.1.call-update) | async-done | bytes 262160 | tf_op jit(solution)/shard_map/psum | solution.py:78
  143.1 13.7 %psum.30 = f32[2,128]{1,0:T(2,128)S(1)} all-reduce(f32[2,128]{1,0:T(2,128)S(1)} %pad_maximum_fusion.2), channel_id=1, replica_groups=mesh['row'=4,'col'=8] {'col'}, use_global_device_ids=true, to_apply=%region_10.0 | all-reduce | flops 256 | bytes 2048 | tf_op jit(solution)/shard_map/psum | solution.py:78
  156.7 10.4 %psum.31 = f32[2,128]{1,0:T(2,128)} all-reduce(f32[2,128]{1,0:T(2,128)S(1)} %psum.30), channel_id=1, replica_groups=mesh['row'=4,'col'=8] {'row'}, use_global_device_ids=true, to_apply=%region_11.0 | all-reduce | flops 256 | bytes 2048 | tf_op jit(solution)/shard_map/psum | solution.py:78
  167.1 0.8 multiply_convert_fusion
  167.9 20.0 %all-reduce.5.cloned.1.call-done = f32[4,128,128]{2,1,0:T(8,128)} async-done(((f32[4,128,128]{2,1,0:T(8,128)}), f32[4,128,128]{2,1,0:T(8,128)}) %all-reduce.5.cloned.1.call-update) | async-done | bytes 262160 | tf_op jit(solution)/shard_map/psum | solution.py:78
  187.9 1.7 copy.41
  (27 shorter events, 0.7 us)
Async XLA Ops:
  7.2 45.6 %reduce-scatter.5.cloned.1.call-start = ((), (), s32[]{:S(2)}) async-start(), calls=%async_computation.3 | async-start | bytes 327680 | tf_op jit(solution)/shard_map/reduce_scatter | solution.py:63
  25.7 1.6 copy-start.2
  27.3 59.1 %reduce-scatter.3.cloned.1.call-start = ((), (), s32[]{:S(2)}) async-start(), calls=%async_computation.2 | async-start | bytes 589824 | tf_op jit(solution)/shard_map/reduce_scatter | solution.py:54
  36.8 2.3 %copy-start = (bf16[1,4,32,128]{3,2,1,0:T(8,128)(2,1)S(1)}, bf16[1,4,32,128]{3,2,1,0:T(8,128)(2,1)}, u32[]{:S(2)}) copy-start(bf16[1,4,32,128]{3,2,1,0:T(8,128)(2,1)} %param.7) | copy-start | bytes 98308
  36.8 2.8 %copy-start.1 = (bf16[4,128,128]{2,1,0:T(8,128)(2,1)S(1)}, bf16[4,128,128]{2,1,0:T(8,128)(2,1)}, u32[]{:S(2)}) copy-start(bf16[4,128,128]{2,1,0:T(8,128)(2,1)} %param.13) | copy-start | bytes 393220
  36.8 2.9 %copy-start.3 = (f32[128]{0:T(128)S(1)}, f32[128]{0:T(128)}, u32[]{:S(2)}) copy-start(f32[128]{0:T(128)} %param.11) | copy-start | bytes 1540
  36.8 2.9 %copy-start.4 = (f32[128]{0:T(128)S(1)}, f32[128]{0:T(128)}, u32[]{:S(2)}) copy-start(f32[128]{0:T(128)} %param.12) | copy-start | bytes 1540
  39.0 104.0 %all-reduce.3.cloned.1.call-start = ((), (), s32[]{:S(2)}) async-start(), calls=%async_computation.4 | async-start | bytes 524288 | tf_op jit(solution)/shard_map/psum | solution.py:78
  88.4 99.5 %all-reduce.5.cloned.1.call-start = ((), (), s32[]{:S(2)}) async-start(), calls=%async_computation.5 | async-start | bytes 524288 | tf_op jit(solution)/shard_map/psum | solution.py:78
Sparse Core Ops, SparseCore 0:
  27.4 25.3 reduce-scatter.4
  55.0 31.3 reduce-scatter.2
  89.3 53.6 all-reduce.2
  145.8 42.0 all-reduce.4
